TPU v7x, 8 devices: a whole 2x2x1 slice. The times are simulated.
8 devices in a mesh: dp: 1 (over z), col: 2 (over y), row: 4 (over x, core).
Axes of the slice: x: 2, y: 2, z: 1, core: 2. Of those that a mesh axis runs over, the one named last changes fastest.
Arguments:
- x_act: bfloat16 [96, 8192], P(('dp', 'row'), 'col')
- ln_gain: float32 [8192], P('col')
- w_in: bfloat16 [8192, 32768], P('row', 'col')
- w_out: bfloat16 [32768, 8192], P('row', 'col')
Outputs:
- output: bfloat16 [96, 8192], P(('dp', 'row'), 'col')
All inputs are finite; a program needn't handle non-finite values.
Results may differ from a plain program's by a relative error of at most 0.00135.
Values are sent between devices in bfloat16 or wider.
A program may use at most 1 GiB of HBM per device.

v0:
```python
import jax
import jax.numpy as jnp
from jax import lax
from jax.sharding import PartitionSpec as P

NORM_EPS = 1e-5


def solution(mesh):
    col_size = mesh.shape["col"]

    def local_block(x_blk, gain_blk, w_in_blk, w_out_blk):
        d_model = x_blk.shape[1] * col_size
        x_f32 = x_blk.astype(jnp.float32)
        part_stats = jnp.stack([jnp.sum(x_f32, axis=1), jnp.sum(x_f32 * x_f32, axis=1)])
        row_stats = lax.psum(part_stats, "col") / d_model
        row_mean = row_stats[0][:, None]
        row_var = row_stats[1][:, None] - row_mean * row_mean
        z_blk = ((x_f32 - row_mean) * lax.rsqrt(row_var + NORM_EPS) * gain_blk).astype(jnp.bfloat16)
        z_rows = lax.all_gather(z_blk, "col", axis=1, tiled=True)
        z_cols = lax.all_to_all(z_rows, "row", 1, 0, tiled=True)
        up_part = jnp.dot(z_cols, w_in_blk, preferred_element_type=jnp.float32)
        up_sum = lax.psum_scatter(up_part, "row", scatter_dimension=0, tiled=True)
        h_blk = jax.nn.gelu(up_sum, approximate=True).astype(jnp.bfloat16)
        h_rows = lax.all_gather(h_blk, "col", axis=1, tiled=True)
        h_cols = lax.all_to_all(h_rows, "row", 1, 0, tiled=True)
        down_part = jnp.dot(h_cols, w_out_blk, preferred_element_type=jnp.float32)
        down_sum = lax.psum_scatter(down_part, "row", scatter_dimension=0, tiled=True)
        return (x_f32 + down_sum).astype(jnp.bfloat16)

    return jax.shard_map(
        local_block,
        mesh=mesh,
        in_specs=(P(("dp", "row"), "col"), P("col"), P("row", "col"), P("row", "col")),
        out_specs=P(("dp", "row"), "col"),
        check_vma=False,
    )
```

profile of v0, /device:TPU:0, one launch (start us, length us, event | category | flops | bytes accessed | tf_op | source)
XLA Modules:
  0.0 214.5 jit_solution(1204191316379360726)
XLA Ops:
  6.5 0.0 reduce-scatter.7.cloned.1.call-start
  6.5 1.1 convert_reduce_fusion
  7.6 6.3 %psum.7 = f32[2,24]{1,0:T(2,128)S(1)} all-reduce(f32[2,24]{1,0:T(2,128)S(1)} %pad_maximum_fusion), channel_id=1, replica_groups=mesh['dp'=1,'col'=2,'row'=4] {'col'}, use_global_device_ids=true, to_apply=%region_2.0 | all-reduce | flops 48 | bytes 384 | tf_op jit(solution)/shard_map/psum | solution.py:16
  13.9 1.1 fusion.11
  15.0 6.5 %all_gather.6 = bf16[24,8192]{1,0:T(8,128)(2,1)S(1)} all-gather(bf16[24,4096]{1,0:T(8,128)(2,1)S(1)} %fusion.11), channel_id=1, replica_groups=mesh['dp'=1,'col'=2,'row'=4] {'col'}, dimensions={1}, use_global_device_ids=true | all-gather | bytes 589824 | tf_op jit(solution)/shard_map/all_gather | solution.py:20
  21.5 10.4 %all_to_all.38 = bf16[24,4,2048]{2,0,1:T(8,128)(2,1)S(1)} all-to-all(bf16[24,4,2048]{2,0,1:T(8,128)(2,1)S(1)} %bitcast.36), channel_id=1, replica_groups=mesh['dp'=1,'col'=2,'row'=4] {'row'}, dimensions={1} | all-to-all | bytes 786432 | tf_op jit(solution)/shard_map/all_to_all | solution.py:21
  31.8 25.8 %fusion.15 = f32[96,16384]{1,0:T(8,128)} fusion(bf16[96,2048]{1,0:T(8,128)(2,1)S(1)} %bitcast.33, bf16[2048,16384]{1,0:T(8,128)(2,1)} %param.6), kind=kOutput, calls=%fused_computation.26 | convolution fusion | flops 6442450944 | bytes 73793536 | tf_op jit(solution)/shard_map/dot_general | solution.py:22
  57.6 0.0 reduce-scatter.7.cloned.1.call-update
  57.6 0.0 all-gather.2.cloned.1.call-start
  57.7 51.5 %reduce-scatter.7.cloned.1.call-done = f32[24,16384]{1,0:T(8,128)} async-done(((f32[96,16384]{1,0:T(8,128)}), f32[24,16384]{1,0:T(8,128)}) %reduce-scatter.7.cloned.1.call-update) | async-done | bytes 1572880
  109.2 2.8 %fusion.7 = bf16[24,16384]{1,0:T(8,128)(2,1)} fusion(f32[24,16384]{1,0:T(8,128)} %reduce-scatter.7.cloned.1.call-done), kind=kLoop, calls=%fused_computation.8 | loop fusion | flops 3538944 | bytes 2359296 | tf_op jit(solution)/shard_map/convert_element_type | solution.py:24
  112.0 0.0 all-gather.2.cloned.1.call-update
  112.0 0.0 reduce-scatter.9.cloned.1.call-start
  112.0 24.2 %all-gather.2.cloned.1.call-done = bf16[24,32768]{1,0:T(8,128)(2,1)} async-done(((bf16[24,16384]{1,0:T(8,128)(2,1)}), bf16[24,32768]{1,0:T(8,128)(2,1)}) %all-gather.2.cloned.1.call-update) | async-done | bytes 1572880 | tf_op jit(solution)/shard_map/all_gather | solution.py:25
  136.3 1.5 copy.15
  137.8 22.6 %all_to_all.39 = bf16[24,4,8192]{2,0,1:T(8,128)(2,1)S(1)} all-to-all(bf16[24,4,8192]{2,0,1:T(8,128)(2,1)S(1)} %bitcast.32), channel_id=1, replica_groups=mesh['dp'=1,'col'=2,'row'=4] {'row'}, dimensions={1} | all-to-all | bytes 3145728 | tf_op jit(solution)/shard_map/all_to_all | solution.py:26
  160.4 24.3 %fusion.16 = f32[96,4096]{1,0:T(8,128)} fusion(bf16[96,8192]{1,0:T(8,128)(2,1)S(1)} %bitcast.31, bf16[8192,4096]{1,0:T(8,128)(2,1)} %param.7), kind=kOutput, calls=%fused_computation.27 | convolution fusion | flops 6442450944 | bytes 70254592 | tf_op jit(solution)/shard_map/dot_general | solution.py:27
  184.6 0.0 copy-start
  184.6 0.0 reduce-scatter.9.cloned.1.call-update
  184.7 21.6 %reduce-scatter.9.cloned.1.call-done = f32[24,4096]{1,0:T(8,128)} async-done(((f32[96,4096]{1,0:T(8,128)}), f32[24,4096]{1,0:T(8,128)}) %reduce-scatter.9.cloned.1.call-update) | async-done | bytes 393232
  206.2 0.0 copy-done
  206.2 1.7 fusion.12
  (5 shorter events, 0.1 us)
Async XLA Ops:
  6.5 102.6 %reduce-scatter.7.cloned.1.call-start = ((), (), s32[]{:S(2)}) async-start(), calls=%async_computation.5 | async-start | bytes 7864320
  57.6 78.6 %all-gather.2.cloned.1.call-start = ((), (), s32[]{:S(2)}) async-start(), calls=%async_computation.4 | async-start | bytes 2359296 | tf_op jit(solution)/shard_map/all_gather | solution.py:25
  112.0 94.3 %reduce-scatter.9.cloned.1.call-start = ((), (), s32[]{:S(2)}) async-start(), calls=%async_computation.6 | async-start | bytes 1966080
  184.6 21.6 %copy-start = (bf16[24,4096]{1,0:T(8,128)(2,1)S(1)}, bf16[24,4096]{1,0:T(8,128)(2,1)}, u32[]{:S(2)}) copy-start(bf16[24,4096]{1,0:T(8,128)(2,1)} %param.4) | copy-start | bytes 589828
Sparse Core Ops, SparseCore 0:
  57.8 51.3 reduce-scatter.6
  112.1 24.1 all-gather.1
  184.8 21.4 reduce-scatter.8
where the time goes:
time: 215 us; the launch traced here: 214 us
  waiting for transfers between devices  97.3 us (45%)
  matrix products  50 us (23%)
  blocking collectives  45.7 us (21%)
  between operations  13.1 us (6%)
  other arithmetic  6.67 us (3%)
    unnamed x5, waiting for transfers between devices  73.1 us
    dot_general x1, matrix products, local_block(): up_part = jnp.dot(z_cols, w_in_blk, preferred_element_type=jnp.float32)  25.8 us
    dot_general x1, matrix products, local_block(): down_part = jnp.dot(h_cols, w_out_blk, preferred_element_type=jnp.float32)  24.3 us
    all_gather x1, waiting for transfers between devices, local_block(): h_rows = lax.all_gather(h_blk, 'col', axis=1, tiled=True)  24.2 us
    all_to_all x1, blocking collectives, local_block(): h_cols = lax.all_to_all(h_rows, 'row', 1, 0, tiled=True)  22.6 us
    all_to_all x1, blocking collectives, local_block(): z_cols = lax.all_to_all(z_rows, 'row', 1, 0, tiled=True)  10.4 us
    all_gather x1, blocking collectives, local_block(): z_rows = lax.all_gather(z_blk, 'col', axis=1, tiled=True)  6.45 us
    psum x1, blocking collectives, local_block(): row_stats = lax.psum(part_stats, 'col') / d_model  6.27 us
  transfers between devices with their start and end apart: 3, of which 3 were waited for; matrix products, arithmetic and copies ran while one was open for 0% of the time, Pallas kernels for 0%

commit v1 on v0

v1 whole, which is shorter than its diff:
```python
import functools
import math

import jax
import jax.numpy as jnp
from jax import lax
from jax.experimental import pallas as pl
from jax.experimental.pallas import tpu as pltpu
from jax.sharding import PartitionSpec as P

NORM_EPS = 1e-5
MESH = pl.DeviceIdType.MESH

TOK = 24
ROWS = 4
T = 16
NB = 32
NA = 40
ND = 24
NU = 5
NDN = 5
LA, LB, LG, LF, LD = 2, 4, 6, 8, 10
FC = 4


def gelu_tanh(v):
    inner = math.sqrt(2.0 / math.pi) * (v + 0.044715 * (v * v * v))
    return v * (0.5 * (1.0 + jnp.tanh(inner)))


def mlp_kernel(
    x_hbm, g_hbm, wi_hbm, wo_hbm, y_ref,
    xv, gv, xblk, gblk, stat, z, usl, dsl, p_own, p_oth, r_d2d, xr, t1, t2, t3, h, hs, acc, dr, fs, xr2,
    ld_s, xs_s, xs_r, g_s, g_r, st_s, st_r, u_sem, d_sem,
    d2d_s, d2d_r, xa_s, xa_r, xb_s, xb_r, t1_s, t1_r, t2_s, t2_r, t3_s, t3_r,
    hb_s, hb_r, hay_s, hay_r, hby_s, hby_r, f_s, f_r, f2_s, f2_r,
):
    r = lax.axis_index("row")
    c = lax.axis_index("col")
    xc = r // 2
    q = r % 2
    home = xc == c
    peer = xc != c
    pair = 2 * xc + (1 - q)
    xrow = 2 * (1 - xc) + q
    ycol = 1 - c
    d_loc = x_hbm.shape[1]
    kdim = z.shape[1]
    w = h.shape[2]
    ntok = ROWS * TOK
    d_model = 2 * d_loc
    half = T * w

    def rcopy(src, dst, ssem, rsem, row, col):
        return pltpu.make_async_remote_copy(
            src_ref=src, dst_ref=dst, send_sem=ssem, recv_sem=rsem,
            device_id={"row": row, "col": col}, device_id_type=MESH)

    ld_x = pltpu.make_async_copy(x_hbm, xv, ld_s.at[0])
    ld_g = pltpu.make_async_copy(g_hbm, gv, ld_s.at[1])
    ld_x.start()
    ld_g.start()

    def u_copy(s, k):
        slot = lax.rem(s, NU)
        side = q if k == 1 else 1 - q
        cols = pl.ds(pl.multiple_of(side * half + s * w, w), w)
        return pltpu.make_async_copy(wi_hbm.at[:, cols], usl.at[slot, k], u_sem.at[slot, k])

    def d_copy(s):
        slot = lax.rem(s, NDN)
        rows = pl.ds(pl.multiple_of(s * w, w), w)
        return pltpu.make_async_copy(wo_hbm.at[rows, :], dsl.at[slot], d_sem.at[slot])

    for s in range(NU):
        u_copy(s, 0).start()
        u_copy(s, 1).start()
    for s in range(NDN):
        d_copy(s).start()

    barrier = pltpu.get_barrier_semaphore()
    for k in range(1, 2 * ROWS):
        rr = lax.rem(r + k, ROWS)
        cc = lax.rem(c + k // ROWS, 2)
        pl.semaphore_signal(barrier, inc=1, device_id={"row": rr, "col": cc}, device_id_type=MESH)
    pl.semaphore_wait(barrier, 2 * ROWS - 1)

    ld_x.wait()

    def x_copy(j, k):
        return rcopy(xv.at[:, pl.ds(j * kdim, kdim)], xblk.at[r], xs_s.at[j, k], xs_r.at[r],
                     2 * c + j, c if k == 0 else ycol)

    for k in (1, 0):
        for j in range(2):
            if k == 1:
                x_copy(j, k).start()
            else:
                @pl.when(2 * c + j != r)
                def _():
                    x_copy(j, k).start()

                @pl.when(2 * c + j == r)
                def _():
                    xblk[2 * c + j] = xv[:, j * kdim:(j + 1) * kdim]

    ld_g.wait()

    def g_copy():
        return rcopy(gv.at[:, pl.ds(pl.multiple_of(q * kdim, kdim), kdim)], gblk, g_s, g_r, r, ycol)

    @pl.when(home)
    def _():
        g_copy().start()
        gblk[...] = gv[:, pl.ds(pl.multiple_of(q * kdim, kdim), kdim)]

    s1 = jnp.zeros((TOK, 128), jnp.float32)
    s2 = jnp.zeros((TOK, 128), jnp.float32)
    for j in range(d_loc // 128):
        v = xv[:, j * 128:(j + 1) * 128].astype(jnp.float32)
        s1 = s1 + v
        s2 = s2 + v * v
    s1 = jnp.sum(s1, axis=1, keepdims=True)
    s2 = jnp.sum(s2, axis=1, keepdims=True)
    lane = lax.broadcasted_iota(jnp.int32, (TOK, 128), 1)
    me = c * ROWS + r
    stat[me] = jnp.where(lane == 0, s1, s2)

    acc[...] = jnp.zeros_like(acc)

    def st_copy(k):
        rr = lax.rem(r + k, ROWS)
        cc = lax.rem(c + k // ROWS, 2)
        return rcopy(stat.at[me], stat.at[me], st_s.at[k], st_r.at[me], rr, cc)

    for k in range(1, 2 * ROWS):
        st_copy(k).start()

    for k in range(1, 2 * ROWS):
        src = lax.rem(c + k // ROWS, 2) * ROWS + lax.rem(r + k, ROWS)
        rcopy(stat.at[src], stat.at[src], st_s.at[k], st_r.at[src], r, ycol).wait_recv()
    for rr in range(ROWS):
        @pl.when(jnp.logical_or(r != rr, peer))
        def _():
            rcopy(xblk.at[rr], xblk.at[rr], xs_s.at[0, 0], xs_r.at[rr], r, ycol).wait_recv()

    @pl.when(peer)
    def _():
        g_copy().wait_recv()

    means, invs = [], []
    for rr in range(ROWS):
        tot = stat[rr] + stat[ROWS + rr]
        mean = tot[:, 0:1] / d_model
        var = tot[:, 1:2] / d_model - mean * mean
        means.append(mean)
        invs.append(lax.rsqrt(var + NORM_EPS))
    zw = 512
    for j in range(kdim // zw):
        cols = slice(j * zw, (j + 1) * zw)
        g = gblk[:, cols]
        parts = []
        for rr in range(ROWS):
            v = xblk[rr, :, cols].astype(jnp.float32)
            parts.append((v - means[rr]) * invs[rr] * g)
        z[:, cols] = jnp.concatenate(parts, axis=0).astype(jnp.bfloat16)

    def d2d(u):
        return rcopy(p_oth.at[u], r_d2d.at[u], d2d_s.at[u], d2d_r.at[u], pair, c)

    def xa(u):
        return rcopy(p_own.at[u, pl.ds(NB, NA)], xr.at[u, pl.ds(0, NA)], xa_s.at[u], xa_r.at[u], xrow, c)

    def xb(u):
        return rcopy(p_own.at[u, pl.ds(0, NB)], xr.at[u, pl.ds(0, NB)], xb_s.at[u], xb_r.at[u], xrow, c)

    def tr1(u):
        return rcopy(p_own.at[u, pl.ds(NB + NA, ND)], t1.at[u], t1_s.at[u], t1_r.at[u], r, ycol)

    def tr2(u):
        return rcopy(t1.at[u], t2.at[u], t2_s.at[u], t2_r.at[u], xrow, c)

    def tr3(u):
        return rcopy(t2.at[u], t3.at[u], t3_s.at[u], t3_r.at[u], r, ycol)

    def hb(u):
        return rcopy(hs.at[u], h.at[u, pl.ds(0, NB)], hb_s.at[u], hb_r.at[u], xrow, c)

    def hay(u):
        rows = pl.ds(NB, ntok - NB)
        return rcopy(h.at[u, rows], h.at[u, rows], hay_s.at[u], hay_r.at[u], r, ycol)

    def hby(u):
        rows = pl.ds(0, NB)
        return rcopy(h.at[u, rows], h.at[u, rows], hby_s.at[u], hby_r.at[u], r, ycol)

    def live(v):
        return jnp.logical_and(v >= 0, v < T)

    def step(s, carry):
        if ND:
            va = s - LA

            @pl.when(jnp.logical_and(live(va), home))
            def _():
                tr1(va).wait_recv()
                tr2(va).start()

            vb = s - LB

            @pl.when(jnp.logical_and(live(vb), peer))
            def _():
                tr2(vb).wait_recv()
                tr3(vb).start()

        vg = s - LG

        @pl.when(jnp.logical_and(live(vg), home))
        def _():
            xa(vg).wait_recv()
            got = xr[vg, 0:NA]
            if ND:
                tr3(vg).wait_recv()
                got = jnp.concatenate([got, t3[vg]], axis=0)
            h[vg, NB:ntok] = gelu_tanh(p_own[vg, NB:ntok] + got).astype(jnp.bfloat16)

        @pl.when(jnp.logical_and(live(vg), peer))
        def _():
            xb(vg).wait_recv()
            hs[vg] = gelu_tanh(p_own[vg, 0:NB] + xr[vg, 0:NB]).astype(jnp.bfloat16)

        slot = lax.rem(s, NU)

        @pl.when(s < T)
        def _():
            u_copy(s, 0).wait()
            p_oth[s] = jnp.dot(z[...], usl[slot, 0], preferred_element_type=jnp.float32)

        @pl.when(jnp.logical_and(live(vg), home))
        def _():
            hay(vg).start()

        @pl.when(jnp.logical_and(live(vg), peer))
        def _():
            hb(vg).start()

        u = s - 1

        @pl.when(live(u))
        def _():
            d2d(u).wait_recv()
            p_own[u] = p_own[u] + r_d2d[u]

        @pl.when(s < T)
        def _():
            d2d(s).start()

        @pl.when(jnp.logical_and(live(u), home))
        def _():
            xb(u).start()

        @pl.when(jnp.logical_and(live(u), peer))
        def _():
            if ND:
                tr1(u).start()
            xa(u).start()

        @pl.when(s < T)
        def _():
            u_copy(s, 1).wait()
            p_own[s] = jnp.dot(z[...], usl[slot, 1], preferred_element_type=jnp.float32)

        @pl.when(s + NU < T)
        def _():
            u_copy(s + NU, 0).start()
            u_copy(s + NU, 1).start()

        vf = s - LF

        @pl.when(jnp.logical_and(live(vf), home))
        def _():
            hb(vf).wait_recv()
            hby(vf).start()

        vd = s - LD

        @pl.when(live(vd))
        def _():
            @pl.when(peer)
            def _():
                hay(vd).wait_recv()
                hby(vd).wait_recv()

            d_copy(vd).wait()
            dslot = lax.rem(vd, NDN)
            hv = h[vd]
            nw = 512
            for n in range(d_loc // nw):
                cols = slice(n * nw, (n + 1) * nw)
                out = jnp.dot(hv, dsl[dslot, :, cols], preferred_element_type=jnp.float32)
                acc[:, :, cols] = acc[:, :, cols] + out.reshape(ROWS, TOK, nw)

            @pl.when(vd + NDN < T)
            def _():
                d_copy(vd + NDN).start()

        return carry

    lax.fori_loop(0, T + LD, step, 0)

    fw = d_loc // FC
    mine_far = 2 * (1 - xc) + q
    pair_far = 2 * (1 - xc) + (1 - q)

    def fcols(k):
        return pl.ds(k * fw, fw)

    def f_copy(i, k):
        tok = pair_far if i == 0 else pair
        return rcopy(acc.at[tok, :, fcols(k)], dr.at[i, :, fcols(k)], f_s.at[i, k], f_r.at[i, k], pair, c)

    def f2_copy(k):
        return rcopy(fs.at[:, fcols(k)], xr2.at[:, fcols(k)], f2_s.at[k], f2_r.at[k], xrow, c)

    for i in range(2):
        for k in range(FC):
            f_copy(i, k).start()
    for k in range(FC):
        cols = slice(k * fw, (k + 1) * fw)
        f_copy(0, k).wait_recv()
        fs[:, cols] = acc[mine_far, :, cols] + dr[0, :, cols]
        if k:
            f2_copy(k - 1).start()
    for k in range(FC):
        cols = slice(k * fw, (k + 1) * fw)
        f_copy(1, k).wait_recv()
        acc[r, :, cols] = acc[r, :, cols] + dr[1, :, cols]
        if k == 0:
            f2_copy(FC - 1).start()

    for k in (1, 0):
        for j in range(2):
            if k == 1:
                x_copy(j, k).wait_send()
            else:
                @pl.when(2 * c + j != r)
                def _():
                    x_copy(j, k).wait_send()

    @pl.when(home)
    def _():
        g_copy().wait_send()

    for k in range(1, 2 * ROWS):
        st_copy(k).wait_send()

    def drain(u, carry):
        d2d(u).wait_send()

        @pl.when(home)
        def _():
            xb(u).wait_send()
            if ND:
                tr2(u).wait_send()
            hay(u).wait_send()
            hby(u).wait_send()

        @pl.when(peer)
        def _():
            xa(u).wait_send()
            if ND:
                tr1(u).wait_send()
                tr3(u).wait_send()
            hb(u).wait_send()

        return carry

    lax.fori_loop(0, T, drain, 0)

    for k in range(FC):
        cols = slice(k * fw, (k + 1) * fw)
        f2_copy(k).wait_recv()
        branch = acc[r, :, cols] + xr2[:, cols]
        y_ref[:, cols] = (xv[:, cols].astype(jnp.float32) + branch).astype(jnp.bfloat16)
    for k in range(FC):
        for i in range(2):
            f_copy(i, k).wait_send()
        f2_copy(k).wait_send()


def solution(mesh):
    def local_block(x_blk, gain_blk, w_in_blk, w_out_blk):
        d_loc = x_blk.shape[1]
        kdim, ff_loc = w_in_blk.shape
        w = ff_loc // (2 * T)
        ntok = ROWS * TOK
        f32, bf16 = jnp.float32, jnp.bfloat16
        dma = pltpu.SemaphoreType.DMA
        nd = max(ND, 8)
        scratch = [
            pltpu.VMEM((TOK, d_loc), bf16),
            pltpu.VMEM((1, d_loc), f32),
            pltpu.VMEM((ROWS, TOK, kdim), bf16),
            pltpu.VMEM((1, kdim), f32),
            pltpu.VMEM((2 * ROWS, TOK, 128), f32),
            pltpu.VMEM((ntok, kdim), bf16),
            pltpu.VMEM((NU, 2, kdim, w), bf16),
            pltpu.VMEM((NDN, w, d_loc), bf16),
            pltpu.VMEM((T, ntok, w), f32),
            pltpu.VMEM((T, ntok, w), f32),
            pltpu.VMEM((T, ntok, w), f32),
            pltpu.VMEM((T, max(NA, NB), w), f32),
            pltpu.VMEM((T, nd, w), f32),
            pltpu.VMEM((T, nd, w), f32),
            pltpu.VMEM((T, nd, w), f32),
            pltpu.VMEM((T, ntok, w), bf16),
            pltpu.VMEM((T, NB, w), bf16),
            pltpu.VMEM((ROWS, TOK, d_loc), f32),
            pltpu.VMEM((2, TOK, d_loc), f32),
            pltpu.VMEM((TOK, d_loc), f32),
            pltpu.VMEM((TOK, d_loc), f32),
            dma((2,)), dma((2, 2)), dma((ROWS,)), dma, dma, dma((2 * ROWS,)), dma((2 * ROWS,)),
            dma((NU, 2)), dma((NDN,)),
        ] + [dma((T,))] * 18 + [dma((2, FC)), dma((2, FC)), dma((FC,)), dma((FC,))]
        return pl.pallas_call(
            mlp_kernel,
            out_shape=jax.ShapeDtypeStruct((TOK, d_loc), bf16),
            in_specs=[pl.BlockSpec(memory_space=pl.ANY)] * 4,
            out_specs=pl.BlockSpec(memory_space=pltpu.VMEM),
            scratch_shapes=scratch,
            compiler_params=pltpu.CompilerParams(
                collective_id=0, has_side_effects=True, vmem_limit_bytes=67_043_328),
        )(x_blk, gain_blk.reshape(1, d_loc), w_in_blk, w_out_blk)

    return jax.shard_map(
        local_block,
        mesh=mesh,
        in_specs=(P(("dp", "row"), "col"), P("col"), P("row", "col"), P("row", "col")),
        out_specs=P(("dp", "row"), "col"),
        check_vma=False,
    )
```

time: 215 us -> 97.5 us (0.45)
  waiting for transfers between devices: 97.3 us -> 0 us
  Pallas kernels: 0 us -> 95.7 us
  matrix products: 50 us -> 0 us
  blocking collectives: 45.7 us -> 0 us
  between operations: 13.1 us -> 0.01 us
  other arithmetic: 6.67 us -> 0 us
    pallas_call x0 -> x1, Pallas kernels: none -> 95.7 us  [local_block(): pl.pallas_call(mlp_kernel, out_shape=jax.ShapeDtypeStruct((TOK, d_loc), b...]
    unnamed x5 -> x0, waiting for transfers between devices: 73.1 us -> none
    dot_general x2 -> x0, matrix products: 50 us -> none  [the longest x1 25.8 us: local_block(): up_part = jnp.dot(z_cols, w_in_blk, preferred_element_type=jnp.float32)]
    all_to_all x2 -> x0, blocking collectives: 33 us -> none  [the longest x1 22.6 us: local_block(): h_cols = lax.all_to_all(h_rows, 'row', 1, 0, tiled=True)]
    all_gather x1 -> x0, waiting for transfers between devices: 24.2 us -> none  [local_block(): h_rows = lax.all_gather(h_blk, 'col', axis=1, tiled=True)]
    all_gather x1 -> x0, blocking collectives: 6.45 us -> none  [local_block(): z_rows = lax.all_gather(z_blk, 'col', axis=1, tiled=True)]
    psum x1 -> x0, blocking collectives: 6.27 us -> none  [local_block(): row_stats = lax.psum(part_stats, 'col') / d_model]
    convert_element_type x3 -> x0, other arithmetic: 5.55 us -> none  [the longest x1 2.79 us: local_block(): h_blk = jax.nn.gelu(up_sum, approximate=True).astype(jnp.bfloat16)]
  transfers between devices with their start and end apart: 3 -> 0, of which waited for: 3 -> 0; matrix products, arithmetic and copies ran while one was open for 0% -> 0% of each run, Pallas kernels for 0% -> 0%
where the time goes in v1:
time: 97.5 us; the launch traced here: 97.4 us
  Pallas kernels  95.7 us (98%)
  local copies, waits for them, and re-layouts  1.62 us (2%)
    pallas_call x1, Pallas kernels, local_block(): pl.pallas_call(mlp_kernel, out_shape=jax.ShapeDtypeStruct((TOK, d_loc), b...  95.7 us

profile of v1, /device:TPU:0, one launch (start us, length us, event | category | flops | bytes accessed | tf_op | source)
XLA Modules:
  0.0 97.4 jit_solution(11686531945259265620)
XLA Ops:
  0.0 95.7 %shard_map.46 = bf16[24,4096]{1,0:T(8,128)(2,1)} custom-call(bf16[24,4096]{1,0:T(8,128)(2,1)} %x_hbm.1, f32[1,4096]{1,0:T(1,128)} %bitcast.1, bf16[2048,16384]{1,0:T(8,128)(2,1)} %wi_hbm.1, bf16[8192,4096]{1,0:T(8,128)(2,1)} %wo_hbm.1), custom_call_target="tpu_custom_call" | custom-call | tf_op jit(solution)/shard_map/pallas_call | solution.py:425
  95.7 1.6 %copy.6 = bf16[24,4096]{1,0:T(8,128)(2,1)} copy(bf16[24,4096]{1,0:T(8,128)(2,1)} %shard_map.46) | data formatting | bytes 393216

commit v2 on v1

--- a/solution.py
+++ b/solution.py
@@ -19,7 +19,12 @@
 ND = 24
 NU = 5
 NDN = 5
-LA, LB, LG, LF, LD = 2, 4, 6, 8, 10
+XRELAY = 3
+LA, LB, LG, LF = 3, 5, 7, 8
+LH, LP = 8, 10
+LX = 3
+TN = T - 1
+NP = 3
 FC = 4
 
 
@@ -30,8 +35,8 @@
 
 def mlp_kernel(
     x_hbm, g_hbm, wi_hbm, wo_hbm, y_ref,
-    xv, gv, xblk, gblk, stat, z, usl, dsl, p_own, p_oth, r_d2d, xr, t1, t2, t3, h, hs, acc, dr, fs, xr2,
-    ld_s, xs_s, xs_r, g_s, g_r, st_s, st_r, u_sem, d_sem,
+    xv, gv, xblk, xrel, gblk, stat, z, usl, dsl, p_own, p_oth, r_d2d, xr, xl, t1, t2, t3, h, hs, acc, dr, fs, xr2,
+    ld_s, xs_s, xs_r, xo_s, xo_r, xl_s, xl_r, hl_s, hl_r, g_s, g_r, st_s, st_r, u_sem, d_sem,
     d2d_s, d2d_r, xa_s, xa_r, xb_s, xb_r, t1_s, t1_r, t2_s, t2_r, t3_s, t3_r,
     hb_s, hb_r, hay_s, hay_r, hby_s, hby_r, f_s, f_r, f2_s, f2_r,
 ):
@@ -61,6 +66,12 @@
     ld_x.start()
     ld_g.start()
 
+    barrier = pltpu.get_barrier_semaphore()
+    for k in range(1, 2 * ROWS):
+        rr = lax.rem(r + k, ROWS)
+        cc = lax.rem(c + k // ROWS, 2)
+        pl.semaphore_signal(barrier, inc=1, device_id={"row": rr, "col": cc}, device_id_type=MESH)
+
     def u_copy(s, k):
         slot = lax.rem(s, NU)
         side = q if k == 1 else 1 - q
@@ -72,47 +83,13 @@
         rows = pl.ds(pl.multiple_of(s * w, w), w)
         return pltpu.make_async_copy(wo_hbm.at[rows, :], dsl.at[slot], d_sem.at[slot])
 
+    ld_x.wait()
+    ld_g.wait()
     for s in range(NU):
         u_copy(s, 0).start()
         u_copy(s, 1).start()
     for s in range(NDN):
         d_copy(s).start()
-
-    barrier = pltpu.get_barrier_semaphore()
-    for k in range(1, 2 * ROWS):
-        rr = lax.rem(r + k, ROWS)
-        cc = lax.rem(c + k // ROWS, 2)
-        pl.semaphore_signal(barrier, inc=1, device_id={"row": rr, "col": cc}, device_id_type=MESH)
-    pl.semaphore_wait(barrier, 2 * ROWS - 1)
-
-    ld_x.wait()
-
-    def x_copy(j, k):
-        return rcopy(xv.at[:, pl.ds(j * kdim, kdim)], xblk.at[r], xs_s.at[j, k], xs_r.at[r],
-                     2 * c + j, c if k == 0 else ycol)
-
-    for k in (1, 0):
-        for j in range(2):
-            if k == 1:
-                x_copy(j, k).start()
-            else:
-                @pl.when(2 * c + j != r)
-                def _():
-                    x_copy(j, k).start()
-
-                @pl.when(2 * c + j == r)
-                def _():
-                    xblk[2 * c + j] = xv[:, j * kdim:(j + 1) * kdim]
-
-    ld_g.wait()
-
-    def g_copy():
-        return rcopy(gv.at[:, pl.ds(pl.multiple_of(q * kdim, kdim), kdim)], gblk, g_s, g_r, r, ycol)
-
-    @pl.when(home)
-    def _():
-        g_copy().start()
-        gblk[...] = gv[:, pl.ds(pl.multiple_of(q * kdim, kdim), kdim)]
 
     s1 = jnp.zeros((TOK, 128), jnp.float32)
     s2 = jnp.zeros((TOK, 128), jnp.float32)
@@ -122,11 +99,23 @@
         s2 = s2 + v * v
     s1 = jnp.sum(s1, axis=1, keepdims=True)
     s2 = jnp.sum(s2, axis=1, keepdims=True)
-    lane = lax.broadcasted_iota(jnp.int32, (TOK, 128), 1)
+    lane = lax.broadcasted_iota(jnp.int32, (8, 128), 1)
     me = c * ROWS + r
-    stat[me] = jnp.where(lane == 0, s1, s2)
-
-    acc[...] = jnp.zeros_like(acc)
+    st = jnp.zeros((8, 128), jnp.float32)
+    for i in range(TOK // 8):
+        st = jnp.where(lane == 2 * i, s1[8 * i:8 * i + 8], st)
+        st = jnp.where(lane == 2 * i + 1, s2[8 * i:8 * i + 8], st)
+    stat[me] = st
+
+    @pl.when(home)
+    def _():
+        gblk[...] = gv[:, pl.ds(pl.multiple_of(q * kdim, kdim), kdim)]
+        for j in range(2):
+            @pl.when(q == j)
+            def _():
+                xblk[r] = xv[:, j * kdim:(j + 1) * kdim]
+
+    pl.semaphore_wait(barrier, 2 * ROWS - 1)
 
     def st_copy(k):
         rr = lax.rem(r + k, ROWS)
@@ -136,13 +125,75 @@
     for k in range(1, 2 * ROWS):
         st_copy(k).start()
 
+    xw = kdim // 2
+
+    def xcols(j, p):
+        return pl.ds(j * kdim + p * xw, xw)
+
+    def xs_home_pair(p):
+        cols = pl.ds(pl.multiple_of((1 - q) * kdim + p * xw, xw), xw)
+        return rcopy(xv.at[:, cols], xblk.at[r, :, pl.ds(p * xw, xw)], xs_s.at[0, p], xs_r.at[r, p], pair, c)
+
+    def xs_home_y(j, p):
+        return rcopy(xv.at[:, xcols(j, p)], xblk.at[r, :, pl.ds(p * xw, xw)], xs_s.at[1 + j, p], xs_r.at[r, p],
+                     2 * xc + j, ycol)
+
+    def xs_peer_x(j, p):
+        return rcopy(xv.at[:, xcols(j, p)], xblk.at[r, :, pl.ds(p * xw, xw)], xs_s.at[j, p], xs_r.at[r, p],
+                     2 * (1 - xc) + j, c)
+
+    def xs_peer_far(j, p):
+        return rcopy(xv.at[:, xcols(j, p)], xblk.at[r, :, pl.ds(p * xw, xw)], xs_s.at[2 + j, p], xs_r.at[r, p],
+                     2 * (1 - xc) + j, ycol)
+
+    def xs_relay_in(j, p):
+        return rcopy(xv.at[:, xcols(j, p)], xrel.at[j, p], xs_s.at[2 + j, p], xo_r.at[j, p], r, ycol)
+
+    def xs_relay_out(j, p):
+        return rcopy(xrel.at[j, p], xblk.at[r, :, pl.ds(p * xw, xw)], xo_s.at[j, p], xs_r.at[r, p],
+                     2 * (1 - xc) + j, c)
+
+    pieces = [(j, p) for p in range(2) for j in range(2)]
+
+    def g_copy():
+        return rcopy(gv.at[:, pl.ds(pl.multiple_of(q * kdim, kdim), kdim)], gblk, g_s, g_r, r, ycol)
+
+    @pl.when(home)
+    def _():
+        for j, p in pieces:
+            xs_home_y(j, p).start()
+        for p in range(2):
+            xs_home_pair(p).start()
+        g_copy().start()
+
+    @pl.when(peer)
+    def _():
+        for n, (j, p) in enumerate(pieces):
+            if n < XRELAY:
+                xs_relay_in(j, p).start()
+            else:
+                xs_peer_far(j, p).start()
+        for j, p in pieces:
+            xs_peer_x(j, p).start()
+
+    acc[...] = jnp.zeros_like(acc)
+
+    @pl.when(home)
+    def _():
+        for n, (j, p) in enumerate(pieces):
+            if n < XRELAY:
+                xs_relay_in(j, p).wait_recv()
+                xs_relay_out(j, p).start()
+
     for k in range(1, 2 * ROWS):
         src = lax.rem(c + k // ROWS, 2) * ROWS + lax.rem(r + k, ROWS)
         rcopy(stat.at[src], stat.at[src], st_s.at[k], st_r.at[src], r, ycol).wait_recv()
-    for rr in range(ROWS):
-        @pl.when(jnp.logical_or(r != rr, peer))
-        def _():
-            rcopy(xblk.at[rr], xblk.at[rr], xs_s.at[0, 0], xs_r.at[rr], r, ycol).wait_recv()
+    for p in range(2):
+        for rr in range(ROWS):
+            @pl.when(jnp.logical_or(r != rr, peer))
+            def _():
+                half_blk = xblk.at[rr, :, pl.ds(p * xw, xw)]
+                rcopy(half_blk, half_blk, xs_s.at[0, 0], xs_r.at[rr, p], r, ycol).wait_recv()
 
     @pl.when(peer)
     def _():
@@ -150,9 +201,9 @@
 
     means, invs = [], []
     for rr in range(ROWS):
-        tot = stat[rr] + stat[ROWS + rr]
-        mean = tot[:, 0:1] / d_model
-        var = tot[:, 1:2] / d_model - mean * mean
+        tot = (stat[rr] + stat[ROWS + rr]) / d_model
+        mean = jnp.concatenate([tot[:, 2 * i:2 * i + 1] for i in range(TOK // 8)], axis=0)
+        var = jnp.concatenate([tot[:, 2 * i + 1:2 * i + 2] for i in range(TOK // 8)], axis=0) - mean * mean
         means.append(mean)
         invs.append(lax.rsqrt(var + NORM_EPS))
     zw = 512
@@ -171,6 +222,12 @@
     def xa(u):
         return rcopy(p_own.at[u, pl.ds(NB, NA)], xr.at[u, pl.ds(0, NA)], xa_s.at[u], xa_r.at[u], xrow, c)
 
+    prow = ntok // NP
+
+    def xl_copy(i):
+        rows = pl.ds(pl.multiple_of(i * prow, prow), prow)
+        return rcopy(p_own.at[TN, rows], xl.at[rows], xl_s.at[i], xl_r.at[i], xrow, c)
+
     def xb(u):
         return rcopy(p_own.at[u, pl.ds(0, NB)], xr.at[u, pl.ds(0, NB)], xb_s.at[u], xb_r.at[u], xrow, c)
 
@@ -190,12 +247,19 @@
         rows = pl.ds(NB, ntok - NB)
         return rcopy(h.at[u, rows], h.at[u, rows], hay_s.at[u], hay_r.at[u], r, ycol)
 
+    def hl_copy(i):
+        rows = pl.ds(pl.multiple_of(i * prow, prow), prow)
+        return rcopy(h.at[TN, rows], h.at[TN, rows], hl_s.at[i], hl_r.at[i], r, ycol)
+
     def hby(u):
         rows = pl.ds(0, NB)
         return rcopy(h.at[u, rows], h.at[u, rows], hby_s.at[u], hby_r.at[u], r, ycol)
 
     def live(v):
-        return jnp.logical_and(v >= 0, v < T)
+        return jnp.logical_and(v >= 0, v < TN)
+
+    def live_piece(i):
+        return jnp.logical_and(i >= 0, i < NP)
 
     def step(s, carry):
         if ND:
@@ -229,6 +293,14 @@
             xb(vg).wait_recv()
             hs[vg] = gelu_tanh(p_own[vg, 0:NB] + xr[vg, 0:NB]).astype(jnp.bfloat16)
 
+        ig = s - T - LX
+
+        @pl.when(jnp.logical_and(live_piece(ig), home))
+        def _():
+            xl_copy(ig).wait_recv()
+            rows = pl.ds(pl.multiple_of(ig * prow, prow), prow)
+            h[TN, rows] = gelu_tanh(p_own[TN, rows] + xl[rows]).astype(jnp.bfloat16)
+
         slot = lax.rem(s, NU)
 
         @pl.when(s < T)
@@ -240,13 +312,17 @@
         def _():
             hay(vg).start()
 
+        @pl.when(jnp.logical_and(live_piece(ig), home))
+        def _():
+            hl_copy(ig).start()
+
         @pl.when(jnp.logical_and(live(vg), peer))
         def _():
             hb(vg).start()
 
         u = s - 1
 
-        @pl.when(live(u))
+        @pl.when(jnp.logical_and(u >= 0, u < T))
         def _():
             d2d(u).wait_recv()
             p_own[u] = p_own[u] + r_d2d[u]
@@ -265,6 +341,10 @@
                 tr1(u).start()
             xa(u).start()
 
+        @pl.when(jnp.logical_and(live_piece(s - T), peer))
+        def _():
+            xl_copy(s - T).start()
+
         @pl.when(s < T)
         def _():
             u_copy(s, 1).wait()
@@ -282,14 +362,19 @@
             hb(vf).wait_recv()
             hby(vf).start()
 
-        vd = s - LD
-
-        @pl.when(live(vd))
-        def _():
-            @pl.when(peer)
+        vd = s - jnp.where(home, LH, LP)
+
+        @pl.when(jnp.logical_and(vd >= 0, vd < T))
+        def _():
+            @pl.when(jnp.logical_and(live(vd), peer))
             def _():
                 hay(vd).wait_recv()
                 hby(vd).wait_recv()
+
+            @pl.when(jnp.logical_and(vd == TN, peer))
+            def _():
+                for i in range(NP):
+                    hl_copy(i).wait_recv()
 
             d_copy(vd).wait()
             dslot = lax.rem(vd, NDN)
@@ -306,7 +391,7 @@
 
         return carry
 
-    lax.fori_loop(0, T + LD, step, 0)
+    lax.fori_loop(0, T + LP, step, 0)
 
     fw = d_loc // FC
     mine_far = 2 * (1 - xc) + q
@@ -338,18 +423,21 @@
         if k == 0:
             f2_copy(FC - 1).start()
 
-    for k in (1, 0):
-        for j in range(2):
-            if k == 1:
-                x_copy(j, k).wait_send()
-            else:
-                @pl.when(2 * c + j != r)
-                def _():
-                    x_copy(j, k).wait_send()
-
     @pl.when(home)
     def _():
+        for j, p in pieces:
+            xs_home_y(j, p).wait_send()
+        for p in range(2):
+            xs_home_pair(p).wait_send()
         g_copy().wait_send()
+        for j, p in pieces[:XRELAY]:
+            xs_relay_out(j, p).wait_send()
+
+    @pl.when(peer)
+    def _():
+        for j, p in pieces:
+            xs_peer_x(j, p).wait_send()
+            xs_peer_far(j, p).wait_send()
 
     for k in range(1, 2 * ROWS):
         st_copy(k).wait_send()
@@ -357,7 +445,7 @@
     def drain(u, carry):
         d2d(u).wait_send()
 
-        @pl.when(home)
+        @pl.when(jnp.logical_and(live(u), home))
         def _():
             xb(u).wait_send()
             if ND:
@@ -365,7 +453,7 @@
             hay(u).wait_send()
             hby(u).wait_send()
 
-        @pl.when(peer)
+        @pl.when(jnp.logical_and(live(u), peer))
         def _():
             xa(u).wait_send()
             if ND:
@@ -376,6 +464,15 @@
         return carry
 
     lax.fori_loop(0, T, drain, 0)
+
+    for i in range(NP):
+        @pl.when(home)
+        def _():
+            hl_copy(i).wait_send()
+
+        @pl.when(peer)
+        def _():
+            xl_copy(i).wait_send()
 
     for k in range(FC):
         cols = slice(k * fw, (k + 1) * fw)
@@ -401,8 +498,9 @@
             pltpu.VMEM((TOK, d_loc), bf16),
             pltpu.VMEM((1, d_loc), f32),
             pltpu.VMEM((ROWS, TOK, kdim), bf16),
+            pltpu.VMEM((2, 2, TOK, kdim // 2), bf16),
             pltpu.VMEM((1, kdim), f32),
-            pltpu.VMEM((2 * ROWS, TOK, 128), f32),
+            pltpu.VMEM((2 * ROWS, 8, 128), f32),
             pltpu.VMEM((ntok, kdim), bf16),
             pltpu.VMEM((NU, 2, kdim, w), bf16),
             pltpu.VMEM((NDN, w, d_loc), bf16),
@@ -410,6 +508,7 @@
             pltpu.VMEM((T, ntok, w), f32),
             pltpu.VMEM((T, ntok, w), f32),
             pltpu.VMEM((T, max(NA, NB), w), f32),
+            pltpu.VMEM((ntok, w), f32),
             pltpu.VMEM((T, nd, w), f32),
             pltpu.VMEM((T, nd, w), f32),
             pltpu.VMEM((T, nd, w), f32),
@@ -419,7 +518,7 @@
             pltpu.VMEM((2, TOK, d_loc), f32),
             pltpu.VMEM((TOK, d_loc), f32),
             pltpu.VMEM((TOK, d_loc), f32),
-            dma((2,)), dma((2, 2)), dma((ROWS,)), dma, dma, dma((2 * ROWS,)), dma((2 * ROWS,)),
+            dma((2,)), dma((4, 2)), dma((ROWS, 2)), dma((2, 2)), dma((2, 2)), dma((NP,)), dma((NP,)), dma((NP,)), dma((NP,)), dma, dma, dma((2 * ROWS,)), dma((2 * ROWS,)),
             dma((NU, 2)), dma((NDN,)),
         ] + [dma((T,))] * 18 + [dma((2, FC)), dma((2, FC)), dma((FC,)), dma((FC,))]
         return pl.pallas_call(

time: 97.5 us -> 83.5 us (0.86)
  Pallas kernels: 95.7 us -> 81.8 us
    pallas_call x1, Pallas kernels: 95.7 us -> 81.8 us  [local_block(): pl.pallas_call(mlp_kernel, out_shape=jax.ShapeDtypeStruct((TOK, d_loc), b...]
where the time goes in v2:
time: 83.5 us; the launch traced here: 83.4 us
  Pallas kernels  81.8 us (98%)
  local copies, waits for them, and re-layouts  1.62 us (2%)
    pallas_call x1, Pallas kernels, local_block(): pl.pallas_call(mlp_kernel, out_shape=jax.ShapeDtypeStruct((TOK, d_loc), b...  81.8 us

profile of v2, /device:TPU:0, one launch (start us, length us, event | category | flops | bytes accessed | tf_op | source)
XLA Modules:
  0.0 83.4 jit_solution(15198417785474227695)
XLA Ops:
  0.0 81.8 %shard_map.46 = bf16[24,4096]{1,0:T(8,128)(2,1)} custom-call(bf16[24,4096]{1,0:T(8,128)(2,1)} %x_hbm.1, f32[1,4096]{1,0:T(1,128)} %bitcast.1, bf16[2048,16384]{1,0:T(8,128)(2,1)} %wi_hbm.1, bf16[8192,4096]{1,0:T(8,128)(2,1)} %wo_hbm.1), custom_call_target="tpu_custom_call" | custom-call | tf_op jit(solution)/shard_map/pallas_call | solution.py:524
  81.8 1.6 %copy.6 = bf16[24,4096]{1,0:T(8,128)(2,1)} copy(bf16[24,4096]{1,0:T(8,128)(2,1)} %shard_map.46) | data formatting | bytes 393216

commit v3 on v2

--- a/solution.py
+++ b/solution.py
@@ -22,7 +22,7 @@
 XRELAY = 3
 LA, LB, LG, LF = 3, 5, 7, 8
 LH, LP = 8, 10
-LX = 3
+LX = 4
 TN = T - 1
 NP = 3
 FC = 4
@@ -36,9 +36,8 @@
 def mlp_kernel(
     x_hbm, g_hbm, wi_hbm, wo_hbm, y_ref,
     xv, gv, xblk, xrel, gblk, stat, z, usl, dsl, p_own, p_oth, r_d2d, xr, xl, t1, t2, t3, h, hs, acc, dr, fs, xr2,
-    ld_s, xs_s, xs_r, xo_s, xo_r, xl_s, xl_r, hl_s, hl_r, g_s, g_r, st_s, st_r, u_sem, d_sem,
-    d2d_s, d2d_r, xa_s, xa_r, xb_s, xb_r, t1_s, t1_r, t2_s, t2_r, t3_s, t3_r,
-    hb_s, hb_r, hay_s, hay_r, hby_s, hby_r, f_s, f_r, f2_s, f2_r,
+    ld_s, xs_s, xs_r, xo_s, xo_r, l_s, xl_r, hl_r, g_s, g_r, st_s, st_r, u_sem, d_sem,
+    d2d_s, d2d_r, x_s, x_r, t_s, t_r, y_s, y_r, b_s, b_r, f_s, f_r, f2_s, f2_r,
 ):
     r = lax.axis_index("row")
     c = lax.axis_index("col")
@@ -120,7 +119,7 @@
     def st_copy(k):
         rr = lax.rem(r + k, ROWS)
         cc = lax.rem(c + k // ROWS, 2)
-        return rcopy(stat.at[me], stat.at[me], st_s.at[k], st_r.at[me], rr, cc)
+        return rcopy(stat.at[me], stat.at[me], st_s, st_r, rr, cc)
 
     for k in range(1, 2 * ROWS):
         st_copy(k).start()
@@ -132,25 +131,25 @@
 
     def xs_home_pair(p):
         cols = pl.ds(pl.multiple_of((1 - q) * kdim + p * xw, xw), xw)
-        return rcopy(xv.at[:, cols], xblk.at[r, :, pl.ds(p * xw, xw)], xs_s.at[0, p], xs_r.at[r, p], pair, c)
+        return rcopy(xv.at[:, cols], xblk.at[r, :, pl.ds(p * xw, xw)], xs_s, xs_r, pair, c)
 
     def xs_home_y(j, p):
-        return rcopy(xv.at[:, xcols(j, p)], xblk.at[r, :, pl.ds(p * xw, xw)], xs_s.at[1 + j, p], xs_r.at[r, p],
+        return rcopy(xv.at[:, xcols(j, p)], xblk.at[r, :, pl.ds(p * xw, xw)], xs_s, xs_r,
                      2 * xc + j, ycol)
 
     def xs_peer_x(j, p):
-        return rcopy(xv.at[:, xcols(j, p)], xblk.at[r, :, pl.ds(p * xw, xw)], xs_s.at[j, p], xs_r.at[r, p],
+        return rcopy(xv.at[:, xcols(j, p)], xblk.at[r, :, pl.ds(p * xw, xw)], xs_s, xs_r,
                      2 * (1 - xc) + j, c)
 
     def xs_peer_far(j, p):
-        return rcopy(xv.at[:, xcols(j, p)], xblk.at[r, :, pl.ds(p * xw, xw)], xs_s.at[2 + j, p], xs_r.at[r, p],
+        return rcopy(xv.at[:, xcols(j, p)], xblk.at[r, :, pl.ds(p * xw, xw)], xs_s, xs_r,
                      2 * (1 - xc) + j, ycol)
 
     def xs_relay_in(j, p):
-        return rcopy(xv.at[:, xcols(j, p)], xrel.at[j, p], xs_s.at[2 + j, p], xo_r.at[j, p], r, ycol)
+        return rcopy(xv.at[:, xcols(j, p)], xrel.at[2 * p + j], xs_s, xo_r.at[j, p], r, ycol)
 
     def xs_relay_out(j, p):
-        return rcopy(xrel.at[j, p], xblk.at[r, :, pl.ds(p * xw, xw)], xo_s.at[j, p], xs_r.at[r, p],
+        return rcopy(xrel.at[2 * p + j], xblk.at[r, :, pl.ds(p * xw, xw)], xo_s, xs_r,
                      2 * (1 - xc) + j, c)
 
     pieces = [(j, p) for p in range(2) for j in range(2)]
@@ -185,15 +184,17 @@
                 xs_relay_in(j, p).wait_recv()
                 xs_relay_out(j, p).start()
 
-    for k in range(1, 2 * ROWS):
-        src = lax.rem(c + k // ROWS, 2) * ROWS + lax.rem(r + k, ROWS)
-        rcopy(stat.at[src], stat.at[src], st_s.at[k], st_r.at[src], r, ycol).wait_recv()
-    for p in range(2):
-        for rr in range(ROWS):
-            @pl.when(jnp.logical_or(r != rr, peer))
-            def _():
-                half_blk = xblk.at[rr, :, pl.ds(p * xw, xw)]
-                rcopy(half_blk, half_blk, xs_s.at[0, 0], xs_r.at[rr, p], r, ycol).wait_recv()
+    others = stat.at[pl.ds(0, 2 * ROWS - 1)]
+    rcopy(others, others, st_s, st_r, r, ycol).wait_recv()
+
+    @pl.when(home)
+    def _():
+        three = xblk.at[pl.ds(0, ROWS - 1)]
+        rcopy(three, three, xs_s, xs_r, r, ycol).wait_recv()
+
+    @pl.when(peer)
+    def _():
+        rcopy(xblk, xblk, xs_s, xs_r, r, ycol).wait_recv()
 
     @pl.when(peer)
     def _():
@@ -217,43 +218,43 @@
         z[:, cols] = jnp.concatenate(parts, axis=0).astype(jnp.bfloat16)
 
     def d2d(u):
-        return rcopy(p_oth.at[u], r_d2d.at[u], d2d_s.at[u], d2d_r.at[u], pair, c)
+        return rcopy(p_oth.at[u], r_d2d.at[u], d2d_s, d2d_r.at[u], pair, c)
 
     def xa(u):
-        return rcopy(p_own.at[u, pl.ds(NB, NA)], xr.at[u, pl.ds(0, NA)], xa_s.at[u], xa_r.at[u], xrow, c)
+        return rcopy(p_own.at[u, pl.ds(NB, NA)], xr.at[u, pl.ds(0, NA)], x_s, x_r.at[u], xrow, c)
 
     prow = ntok // NP
 
     def xl_copy(i):
         rows = pl.ds(pl.multiple_of(i * prow, prow), prow)
-        return rcopy(p_own.at[TN, rows], xl.at[rows], xl_s.at[i], xl_r.at[i], xrow, c)
+        return rcopy(p_own.at[TN, rows], xl.at[rows], l_s, xl_r.at[i], xrow, c)
 
     def xb(u):
-        return rcopy(p_own.at[u, pl.ds(0, NB)], xr.at[u, pl.ds(0, NB)], xb_s.at[u], xb_r.at[u], xrow, c)
+        return rcopy(p_own.at[u, pl.ds(0, NB)], xr.at[u, pl.ds(0, NB)], x_s, x_r.at[u], xrow, c)
 
     def tr1(u):
-        return rcopy(p_own.at[u, pl.ds(NB + NA, ND)], t1.at[u], t1_s.at[u], t1_r.at[u], r, ycol)
+        return rcopy(p_own.at[u, pl.ds(NB + NA, ND)], t1.at[u], t_s, t_r.at[u], r, ycol)
 
     def tr2(u):
-        return rcopy(t1.at[u], t2.at[u], t2_s.at[u], t2_r.at[u], xrow, c)
+        return rcopy(t1.at[u], t2.at[u], t_s, t_r.at[u], xrow, c)
 
     def tr3(u):
-        return rcopy(t2.at[u], t3.at[u], t3_s.at[u], t3_r.at[u], r, ycol)
+        return rcopy(t2.at[u], t3.at[u], y_s, y_r.at[u], r, ycol)
 
     def hb(u):
-        return rcopy(hs.at[u], h.at[u, pl.ds(0, NB)], hb_s.at[u], hb_r.at[u], xrow, c)
+        return rcopy(hs.at[u], h.at[u, pl.ds(0, NB)], b_s, b_r.at[u], xrow, c)
 
     def hay(u):
         rows = pl.ds(NB, ntok - NB)
-        return rcopy(h.at[u, rows], h.at[u, rows], hay_s.at[u], hay_r.at[u], r, ycol)
+        return rcopy(h.at[u, rows], h.at[u, rows], y_s, y_r.at[u], r, ycol)
 
     def hl_copy(i):
         rows = pl.ds(pl.multiple_of(i * prow, prow), prow)
-        return rcopy(h.at[TN, rows], h.at[TN, rows], hl_s.at[i], hl_r.at[i], r, ycol)
+        return rcopy(h.at[TN, rows], h.at[TN, rows], l_s, hl_r, r, ycol)
 
     def hby(u):
         rows = pl.ds(0, NB)
-        return rcopy(h.at[u, rows], h.at[u, rows], hby_s.at[u], hby_r.at[u], r, ycol)
+        return rcopy(h.at[u, rows], h.at[u, rows], b_s, b_r.at[u], r, ycol)
 
     def live(v):
         return jnp.logical_and(v >= 0, v < TN)
@@ -262,21 +263,6 @@
         return jnp.logical_and(i >= 0, i < NP)
 
     def step(s, carry):
-        if ND:
-            va = s - LA
-
-            @pl.when(jnp.logical_and(live(va), home))
-            def _():
-                tr1(va).wait_recv()
-                tr2(va).start()
-
-            vb = s - LB
-
-            @pl.when(jnp.logical_and(live(vb), peer))
-            def _():
-                tr2(vb).wait_recv()
-                tr3(vb).start()
-
         vg = s - LG
 
         @pl.when(jnp.logical_and(live(vg), home))
@@ -320,6 +306,21 @@
         def _():
             hb(vg).start()
 
+        if ND:
+            va = s - LA
+
+            @pl.when(jnp.logical_and(live(va), home))
+            def _():
+                tr1(va).wait_recv()
+                tr2(va).start()
+
+            vb = s - LB
+
+            @pl.when(jnp.logical_and(live(vb), peer))
+            def _():
+                tr2(vb).wait_recv()
+                tr3(vb).start()
+
         u = s - 1
 
         @pl.when(jnp.logical_and(u >= 0, u < T))
@@ -373,8 +374,7 @@
 
             @pl.when(jnp.logical_and(vd == TN, peer))
             def _():
-                for i in range(NP):
-                    hl_copy(i).wait_recv()
+                rcopy(h.at[TN], h.at[TN], l_s, hl_r, r, ycol).wait_recv()
 
             d_copy(vd).wait()
             dslot = lax.rem(vd, NDN)
@@ -402,10 +402,10 @@
 
     def f_copy(i, k):
         tok = pair_far if i == 0 else pair
-        return rcopy(acc.at[tok, :, fcols(k)], dr.at[i, :, fcols(k)], f_s.at[i, k], f_r.at[i, k], pair, c)
+        return rcopy(acc.at[tok, :, fcols(k)], dr.at[i, :, fcols(k)], f_s, f_r.at[i, k], pair, c)
 
     def f2_copy(k):
-        return rcopy(fs.at[:, fcols(k)], xr2.at[:, fcols(k)], f2_s.at[k], f2_r.at[k], xrow, c)
+        return rcopy(fs.at[:, fcols(k)], xr2.at[:, fcols(k)], f2_s, f2_r.at[k], xrow, c)
 
     for i in range(2):
         for k in range(FC):
@@ -423,66 +423,39 @@
         if k == 0:
             f2_copy(FC - 1).start()
 
+    def all_sent(ref, sem):
+        rcopy(ref, ref, sem, d2d_r.at[0], pair, c).wait_send()
+
+    allc = pl.ds(0, TN)
+    all_sent(p_oth, d2d_s)
+    all_sent(others, st_s)
+
     @pl.when(home)
     def _():
-        for j, p in pieces:
-            xs_home_y(j, p).wait_send()
-        for p in range(2):
-            xs_home_pair(p).wait_send()
+        all_sent(xblk.at[pl.ds(0, ROWS - 1)], xs_s)
+        all_sent(xrel.at[pl.ds(0, XRELAY)], xo_s)
         g_copy().wait_send()
-        for j, p in pieces[:XRELAY]:
-            xs_relay_out(j, p).wait_send()
+        all_sent(h.at[TN], l_s)
+        all_sent(p_own.at[allc, pl.ds(0, NB)], x_s)
+        all_sent(h.at[allc, pl.ds(NB, ntok - NB)], y_s)
 
     @pl.when(peer)
     def _():
-        for j, p in pieces:
-            xs_peer_x(j, p).wait_send()
-            xs_peer_far(j, p).wait_send()
-
-    for k in range(1, 2 * ROWS):
-        st_copy(k).wait_send()
-
-    def drain(u, carry):
-        d2d(u).wait_send()
-
-        @pl.when(jnp.logical_and(live(u), home))
-        def _():
-            xb(u).wait_send()
-            if ND:
-                tr2(u).wait_send()
-            hay(u).wait_send()
-            hby(u).wait_send()
-
-        @pl.when(jnp.logical_and(live(u), peer))
-        def _():
-            xa(u).wait_send()
-            if ND:
-                tr1(u).wait_send()
-                tr3(u).wait_send()
-            hb(u).wait_send()
-
-        return carry
-
-    lax.fori_loop(0, T, drain, 0)
-
-    for i in range(NP):
-        @pl.when(home)
-        def _():
-            hl_copy(i).wait_send()
-
-        @pl.when(peer)
-        def _():
-            xl_copy(i).wait_send()
+        all_sent(xblk, xs_s)
+        all_sent(p_own.at[TN], l_s)
+        all_sent(p_own.at[allc, pl.ds(NB, NA)], x_s)
+        all_sent(t3.at[allc], y_s)
+
+    all_sent(t1.at[allc], t_s)
+    all_sent(h.at[allc, pl.ds(0, NB)], b_s)
 
     for k in range(FC):
         cols = slice(k * fw, (k + 1) * fw)
         f2_copy(k).wait_recv()
         branch = acc[r, :, cols] + xr2[:, cols]
         y_ref[:, cols] = (xv[:, cols].astype(jnp.float32) + branch).astype(jnp.bfloat16)
-    for k in range(FC):
-        for i in range(2):
-            f_copy(i, k).wait_send()
-        f2_copy(k).wait_send()
+    all_sent(dr, f_s)
+    all_sent(fs, f2_s)
 
 
 def solution(mesh):
@@ -498,7 +471,7 @@
             pltpu.VMEM((TOK, d_loc), bf16),
             pltpu.VMEM((1, d_loc), f32),
             pltpu.VMEM((ROWS, TOK, kdim), bf16),
-            pltpu.VMEM((2, 2, TOK, kdim // 2), bf16),
+            pltpu.VMEM((4, TOK, kdim // 2), bf16),
             pltpu.VMEM((1, kdim), f32),
             pltpu.VMEM((2 * ROWS, 8, 128), f32),
             pltpu.VMEM((ntok, kdim), bf16),
@@ -518,9 +491,9 @@
             pltpu.VMEM((2, TOK, d_loc), f32),
             pltpu.VMEM((TOK, d_loc), f32),
             pltpu.VMEM((TOK, d_loc), f32),
-            dma((2,)), dma((4, 2)), dma((ROWS, 2)), dma((2, 2)), dma((2, 2)), dma((NP,)), dma((NP,)), dma((NP,)), dma((NP,)), dma, dma, dma((2 * ROWS,)), dma((2 * ROWS,)),
+            dma((2,)), dma, dma, dma, dma((2, 2)), dma, dma((NP,)), dma, dma, dma, dma, dma,
             dma((NU, 2)), dma((NDN,)),
-        ] + [dma((T,))] * 18 + [dma((2, FC)), dma((2, FC)), dma((FC,)), dma((FC,))]
+        ] + [dma, dma((T,))] + [dma, dma((TN,))] * 4 + [dma, dma((2, FC)), dma, dma((FC,))]
         return pl.pallas_call(
             mlp_kernel,
             out_shape=jax.ShapeDtypeStruct((TOK, d_loc), bf16),

time: 83.5 us -> 80.4 us (0.963)
  Pallas kernels: 81.8 us -> 78.6 us
    pallas_call x1, Pallas kernels: 81.8 us -> 78.6 us  [local_block(): pl.pallas_call(mlp_kernel, out_shape=jax.ShapeDtypeStruct((TOK, d_loc), b...]
where the time goes in v3:
time: 80.4 us; the launch traced here: 80.3 us
  Pallas kernels  78.6 us (98%)
  local copies, waits for them, and re-layouts  1.62 us (2%)
    pallas_call x1, Pallas kernels, local_block(): pl.pallas_call(mlp_kernel, out_shape=jax.ShapeDtypeStruct((TOK, d_loc), b...  78.6 us
    unnamed x1, local copies, waits for them, and re-layouts  1.62 us

profile of v3, /device:TPU:0, one launch (start us, length us, event | category | flops | bytes accessed | tf_op | source)
XLA Modules:
  0.0 80.3 jit_solution(10877677431310465952)
XLA Ops:
  0.0 78.6 %shard_map.46 = bf16[24,4096]{1,0:T(8,128)(2,1)} custom-call(bf16[24,4096]{1,0:T(8,128)(2,1)} %x_hbm.1, f32[1,4096]{1,0:T(1,128)} %bitcast.1, bf16[2048,16384]{1,0:T(8,128)(2,1)} %wi_hbm.1, bf16[8192,4096]{1,0:T(8,128)(2,1)} %wo_hbm.1), custom_call_target="tpu_custom_call" | custom-call | tf_op jit(solution)/shard_map/pallas_call | solution.py:497
  78.6 1.6 %copy.6 = bf16[24,4096]{1,0:T(8,128)(2,1)} copy(bf16[24,4096]{1,0:T(8,128)(2,1)} %shard_map.46) | data formatting | bytes 393216

commit v4 on v3

--- a/solution.py
+++ b/solution.py
@@ -21,11 +21,11 @@
 NDN = 5
 XRELAY = 3
 LA, LB, LG, LF = 3, 5, 7, 8
-LH, LP = 8, 10
-LX = 4
+LH, LP = 9, 10
+LX = 6
 TN = T - 1
 NP = 3
-FC = 4
+FC = 2
 
 
 def gelu_tanh(v):
@@ -491,11 +491,17 @@
             pltpu.VMEM((2, TOK, d_loc), f32),
             pltpu.VMEM((TOK, d_loc), f32),
             pltpu.VMEM((TOK, d_loc), f32),
+        ]
+        semaphores = [
             dma((2,)), dma, dma, dma, dma((2, 2)), dma, dma((NP,)), dma, dma, dma, dma, dma,
             dma((NU, 2)), dma((NDN,)),
         ] + [dma, dma((T,))] + [dma, dma((TN,))] * 4 + [dma, dma((2, FC)), dma, dma((FC,))]
+
+        def scoped_kernel(*refs):
+            pl.run_scoped(lambda *sems: mlp_kernel(*refs, *sems), *semaphores)
+
         return pl.pallas_call(
-            mlp_kernel,
+            scoped_kernel,
             out_shape=jax.ShapeDtypeStruct((TOK, d_loc), bf16),
             in_specs=[pl.BlockSpec(memory_space=pl.ANY)] * 4,
             out_specs=pl.BlockSpec(memory_space=pltpu.VMEM),

time: 80.4 us -> 78.3 us (0.974)
  Pallas kernels: 78.6 us -> 76.5 us
    pallas_call x1, Pallas kernels: 78.6 us -> 76.5 us  [local_block(): pl.pallas_call(scoped_kernel, out_shape=jax.ShapeDtypeStruct((TOK, d_loc)...]
where the time goes in v4:
time: 78.3 us; the launch traced here: 78.1 us
  Pallas kernels  76.5 us (98%)
  local copies, waits for them, and re-layouts  1.62 us (2%)
    pallas_call x1, Pallas kernels, local_block(): pl.pallas_call(scoped_kernel, out_shape=jax.ShapeDtypeStruct((TOK, d_loc)...  76.5 us
    unnamed x1, local copies, waits for them, and re-layouts  1.62 us

profile of v4, /device:TPU:0, one launch (start us, length us, event | category | flops | bytes accessed | tf_op | source)
XLA Modules:
  0.0 78.1 jit_solution(5506020977967720483)
XLA Ops:
  0.0 76.5 %shard_map.46 = bf16[24,4096]{1,0:T(8,128)(2,1)} custom-call(bf16[24,4096]{1,0:T(8,128)(2,1)} %refs_0_.1, f32[1,4096]{1,0:T(1,128)} %bitcast.1, bf16[2048,16384]{1,0:T(8,128)(2,1)} %refs_2_.1, bf16[8192,4096]{1,0:T(8,128)(2,1)} %refs_3_.1), custom_call_target="tpu_custom_call" | custom-call | tf_op jit(solution)/shard_map/pallas_call | solution.py:503
  76.5 1.6 %copy.6 = bf16[24,4096]{1,0:T(8,128)(2,1)} copy(bf16[24,4096]{1,0:T(8,128)(2,1)} %shard_map.46) | data formatting | bytes 393216

commit v5 on v4

--- a/solution.py
+++ b/solution.py
@@ -20,7 +20,7 @@
 NU = 5
 NDN = 5
 XRELAY = 3
-LA, LB, LG, LF = 3, 5, 7, 8
+LA, LB, LG, LF = 4, 6, 7, 8
 LH, LP = 9, 10
 LX = 6
 TN = T - 1
@@ -356,13 +356,6 @@
             u_copy(s + NU, 0).start()
             u_copy(s + NU, 1).start()
 
-        vf = s - LF
-
-        @pl.when(jnp.logical_and(live(vf), home))
-        def _():
-            hb(vf).wait_recv()
-            hby(vf).start()
-
         vd = s - jnp.where(home, LH, LP)
 
         @pl.when(jnp.logical_and(vd >= 0, vd < T))
@@ -388,6 +381,13 @@
             @pl.when(vd + NDN < T)
             def _():
                 d_copy(vd + NDN).start()
+
+        vf = s - LF
+
+        @pl.when(jnp.logical_and(live(vf), home))
+        def _():
+            hb(vf).wait_recv()
+            hby(vf).start()
 
         return carry
 

time: 78.3 us -> 78.1 us (level)
  no operation moved by 1% of the time
where the time goes in v5:
time: 78.1 us; the launch traced here: 78 us
  Pallas kernels  76.3 us (98%)
  local copies, waits for them, and re-layouts  1.62 us (2%)
    pallas_call x1, Pallas kernels, local_block(): pl.pallas_call(scoped_kernel, out_shape=jax.ShapeDtypeStruct((TOK, d_loc)...  76.3 us
    unnamed x1, local copies, waits for them, and re-layouts  1.62 us

profile of v5, /device:TPU:0, one launch (start us, length us, event | category | flops | bytes accessed | tf_op | source)
XLA Modules:
  0.0 78.0 jit_solution(11356588873556863910)
XLA Ops:
  0.0 76.3 %shard_map.46 = bf16[24,4096]{1,0:T(8,128)(2,1)} custom-call(bf16[24,4096]{1,0:T(8,128)(2,1)} %refs_0_.1, f32[1,4096]{1,0:T(1,128)} %bitcast.1, bf16[2048,16384]{1,0:T(8,128)(2,1)} %refs_2_.1, bf16[8192,4096]{1,0:T(8,128)(2,1)} %refs_3_.1), custom_call_target="tpu_custom_call" | custom-call | tf_op jit(solution)/shard_map/pallas_call | solution.py:503
  76.3 1.6 %copy.6 = bf16[24,4096]{1,0:T(8,128)(2,1)} copy(bf16[24,4096]{1,0:T(8,128)(2,1)} %shard_map.46) | data formatting | bytes 393216
